TPU v7x, 1024 devices: a whole 4x8x16 slice. The times are simulated.
1024 devices in a mesh: slab: 16 (over z), swap: 64 (over x, y, core).
Axes of the slice: x: 4, y: 8, z: 16, core: 2. Of those that a mesh axis runs over, the one named last changes fastest.
Arguments:
- fluid_state: float32 [2, 4096, 128, 256], P(None, ('slab', 'swap')), may hold values from -0.45 to 1.6, as said below
- material: int32 [4096, 128, 256], P(('slab', 'swap')), may hold values from 0 to 7
- table_colour: float32 [3, 8], replicated, may hold values from 0.2 to 2
- table_extinction: float32 [8], replicated, may hold values from 0.2 to 1.5
Outputs:
- new_density: float32 [4096, 128, 256], P(('slab', 'swap'))
- rendered: float32 [4, 32768], P(None, 'swap')
Inputs may be any that keep to these rules, and one draw needn't show every extreme that they name: fluid_state[0] is the density, between 0.6 and 1.6; fluid_state[1] is the momentum along the view axis, between -0.45 and 0.45.
All inputs are finite; a program needn't handle non-finite values.
Results may differ from a plain program's by a relative error of at most 0.0003.
Values sent between devices are 32-bit elements; how exact they have to be, the bound alone decides.
A program may use at most 32 MiB of HBM per device.

v0:
```python
import jax
import jax.numpy as jnp
from jax import lax
from jax.sharding import PartitionSpec as P

COURANT = 0.4
DEPTH_SCALE = 2.5


def padded(array, sides, width):
    edges = {}
    for axis, dim in sides:
        devices, length = (lax.axis_size(axis), array.shape[dim])
        up = [(i, (i + 1) % devices) for i in range(devices)]
        last = lax.slice_in_dim(array, length - width, length, axis=dim)
        leading = lax.slice_in_dim(array, 0, width, axis=dim)
        edges[dim] = (
            lax.ppermute(last, axis, up),
            lax.ppermute(leading, axis, [(b, a) for a, b in up]),
        )
    done = []
    for _, dim in sides:
        low, high = edges[dim]
        around = [(width, width) if d in done else (0, 0) for d in range(array.ndim)]
        array = jnp.concatenate([jnp.pad(low, around), array, jnp.pad(high, around)], axis=dim)
        done.append(dim)
    return array


def in_order(parts, dim):
    dims = list(parts.shape[1:])
    dims[dim] *= parts.shape[0]
    return jnp.moveaxis(parts, 0, dim).reshape(dims)


def sent_to_all(array, axis):
    devices = lax.axis_size(axis)
    return lax.all_to_all(
        jnp.broadcast_to(array[None], (devices, *array.shape)), axis, 0, 0, tiled=True
    )


def collect(array, axis, dim):
    return in_order(sent_to_all(array, axis), dim)


def hydro_step(fields):
    density = fields[0]
    momentum = fields[1]
    velocity = momentum / density
    speeds = jnp.abs(velocity) + 1.0
    fluxes = jnp.stack([momentum, momentum * velocity + density])
    face_speed = jnp.maximum(speeds[:-1], speeds[1:])
    face_flux = 0.5 * (fluxes[:, :-1] + fluxes[:, 1:]) - 0.5 * face_speed * (
        fields[:, 1:] - fields[:, :-1]
    )
    return fields[:, 1:-1] - COURANT * (face_flux[:, 1:] - face_flux[:, :-1])


def stack_over(pieces):
    through = jnp.cumprod(1.0 - pieces[3], axis=0)
    before = jnp.concatenate([jnp.ones_like(through[:1]), through[:-1]], axis=0)
    colour = jnp.sum(before[None] * pieces[:3], axis=1)
    opacity = 1.0 - through[-1]
    return jnp.concatenate([colour, opacity[None]], axis=0)


def render_local(density, material, table_colour, table_extinction, total_cells):
    extinction = jnp.zeros(density.shape, jnp.float32)
    for number in range(table_extinction.shape[0]):
        extinction = extinction + jnp.where(material == number, table_extinction[number], 0.0)
    optical = DEPTH_SCALE * extinction * density / total_cells
    running = jnp.cumsum(optical, axis=0)
    weight = jnp.exp(optical - running) * (1.0 - jnp.exp(-optical))
    colour = jnp.zeros((3,) + density.shape[1:], jnp.float32)
    for number in range(table_extinction.shape[0]):
        summed = jnp.sum(jnp.where(material == number, weight, 0.0), axis=0)
        colour = colour + table_colour[:, number][:, None, None] * summed[None]
    opacity = 1.0 - jnp.exp(-running[-1])
    return jnp.concatenate([colour, opacity[None]], axis=0)


def per_device(fluid_state, material, table_colour, table_extinction):
    slabs = lax.axis_size("slab")
    members = lax.axis_size("swap")
    depth_cells = fluid_state.shape[1]
    fields = padded(fluid_state, ((("slab", "swap"), 1),), 4)
    for number in range(4):
        fields = hydro_step(fields)
    density = fields[0]
    local = render_local(
        density, material, table_colour, table_extinction, depth_cells * slabs * members
    )
    pixels = local.shape[1] * local.shape[2]
    tile_width = pixels // members
    holding = local.reshape(4, members, tile_width)
    received = lax.all_to_all(holding, "swap", split_axis=1, concat_axis=1, tiled=True)
    group_tile = stack_over(received)[:, None, :]
    every_group = collect(group_tile, "slab", 1)
    return (density, stack_over(every_group))


def solution(mesh):
    return jax.shard_map(
        per_device,
        mesh=mesh,
        in_specs=(P(None, ("slab", "swap"), None, None), P(("slab", "swap"), None, None), P(), P()),
        out_specs=(P(("slab", "swap"), None, None), P(None, "swap")),
        check_vma=False,
    )
```

profile of v0, /device:TPU:6, one launch (start us, length us, event | category | flops | bytes accessed | tf_op | source)
XLA Modules:
  0.0 100.1 jit_solution(7776385896886324233)
XLA Ops:
  0.6 0.0 copy-start.1
  0.6 2.1 %collective-permute-start = (f32[2,4,128,256]{3,2,1,0:T(8,128)}, f32[2,4,128,256]{3,2,1,0:T(8,128)S(1)}, u32[]{:S(2)}, u32[]{:S(2)}) collective-permute-start(f32[2,4,128,256]{3,2,1,0:T(8,128)} %param.4), channel_id=1, source_target_pairs={{0,1},{1,2},{2,3},{3,4},{4,5},{5,6},{6,7},{7,8},{8,9},{9,10},{10,1... | collective-permute-start | bytes 3145736 | tf_op jit(solution)/shard_map/ppermute | solution.py:18
  2.7 5.8 %collective-permute-start.1 = (f32[2,4,128,256]{3,2,1,0:T(8,128)}, f32[2,4,128,256]{3,2,1,0:T(8,128)S(1)}, u32[]{:S(2)}, u32[]{:S(2)}) collective-permute-start(f32[2,4,128,256]{3,2,1,0:T(8,128)} %param.4), channel_id=1, source_target_pairs={{1,0},{2,1},{3,2},{4,3},{5,4},{6,5},{7,6},{8,7},{9,8},{10,9},{11,1... | collective-permute-start | bytes 3145736 | tf_op jit(solution)/shard_map/ppermute | solution.py:19
  8.5 1.6 %fusion.44 = (f32[1]{0:T(128)}, f32[1]{0:T(128)}, f32[1]{0:T(128)}, f32[1]{0:T(128)}, f32[1]{0:T(128)}, /*index=5*/f32[1]{0:T(128)}, f32[1]{0:T(128)}, f32[1]{0:T(128)}) fusion(f32[8]{0:T(128)} %param.7), kind=kLoop, calls=%fused_computation.122 | loop fusion | bytes 64 | tf_op jit(solution)/shard_map/slice | solution.py:71
  10.1 1.3 %slice_reduce_fusion.7 = (f32[3]{0:T(128)S(1)}, f32[3]{0:T(128)S(1)}, f32[3]{0:T(128)S(1)}, f32[3]{0:T(128)S(1)}, f32[3]{0:T(128)S(1)}, /*index=5*/f32[3]{0:T(128)S(1)}, f32[3]{0:T(128)S(1)}, f32[3]{0:T(128)S(1)}) fusion(f32[3,8]{1,0:T(4,128)} %param.6), kind=kLoop, calls=%fused_computation.120 | loop fusion | bytes 192 | tf_op jit(solution)/shard_map/slice | solution.py:78
  11.4 7.8 %collective-permute-done = f32[2,4,128,256]{3,2,1,0:T(8,128)S(1)} collective-permute-done((f32[2,4,128,256]{3,2,1,0:T(8,128)}, f32[2,4,128,256]{3,2,1,0:T(8,128)S(1)}, u32[]{:S(2)}, u32[]{:S(2)}) %collective-permute-start) | collective-permute-done | bytes 1048608 | tf_op jit(solution)/shard_map/ppermute | solution.py:18
  19.2 0.1 constant_dynamic-update-slice_fusion.2
  19.3 0.0 copy-done.1
  19.3 0.1 constant_dynamic-update-slice_fusion.1
  19.4 1.7 %collective-permute-done.1 = f32[2,4,128,256]{3,2,1,0:T(8,128)S(1)} collective-permute-done((f32[2,4,128,256]{3,2,1,0:T(8,128)}, f32[2,4,128,256]{3,2,1,0:T(8,128)S(1)}, u32[]{:S(2)}, u32[]{:S(2)}) %collective-permute-start.1) | collective-permute-done | bytes 1048608 | tf_op jit(solution)/shard_map/ppermute | solution.py:19
  21.1 0.1 constant_dynamic-update-slice_fusion
  21.1 0.5 abs_add_fusion
  21.6 0.1 fusion.22
  21.7 1.3 %fusion.3 = f32[2,11,128,256]{3,2,1,0:T(8,128)S(1)} fusion(f32[1,12,128,256]{3,2,1,0:T(8,128)S(1)} %get-tuple-element.30, f32[1,12,128,256]{3,2,1,0:T(8,128)S(1)} %get-tuple-element.29, f32[2,12,128,256]{3,2,1,0:T(8,128)S(1)} %constant_dynamic-update-slice_fusion, f32[11,128,256]{2,1,0:T(8,128)S(1)} %fusion.22), kind=kLoop, calls=%fused_computation.5 | loop fusion | flops 5046272 | bytes 13238272 | tf_op jit(solution)/shard_map/sub | solution.py:54
  23.0 0.4 fusion.6
  23.4 0.4 abs_add_fusion.1
  23.9 0.1 fusion.29
  24.0 0.6 fusion.10
  24.6 0.4 fusion.13
  25.0 0.3 abs_add_fusion.2
  25.3 0.1 fusion.31
  25.4 0.4 fusion.17
  25.7 0.3 fusion.20
  26.0 0.0 copy-start
  26.0 0.2 abs_add_fusion.3
  26.3 0.1 fusion.33
  26.3 0.9 copy-done
  27.2 0.3 fusion.26
  27.4 0.0 slice-start
  27.4 0.0 copy-start.2
  27.5 0.2 fusion.43
  27.7 1.0 slice-done
  28.7 0.1 copy-done.2
  28.8 6.7 %multiply_multiply_fusion = (f32[4,128,256]{2,1,0:T(8,128)S(1)}, pred[4,128,256]{2,1,0:T(8,128)(4,1)S(1)}, pred[4,128,256]{2,1,0:T(8,128)(4,1)S(1)}, pred[4,128,...) fusion(f32[]{:T(128)} %bitcast.12, f32[]{:T(128)} %bitcast.11, ...), kind=kLoop, calls=%fused_computation.86 | loop fusion | flops 3801088 | bytes 4194336 | tf_op jit(solution)/shard_map/div | solution.py:72
  35.5 0.3 fusion.45
  35.8 0.7 select_reduce_fusion.7
  36.9 0.1 concatenate.22
  37.0 0.6 multiply_add_fusion.4
  37.6 0.2 pad_maximum_fusion.4
  37.9 37.7 %all_to_all.10 = f32[4,64,512]{2,0,1:T(4,128)S(1)} all-to-all(f32[4,64,512]{2,0,1:T(4,128)S(1)} %pad_maximum_fusion.4), channel_id=1, replica_groups=mesh['slab'=16,'swap'=64] {'swap'}, dimensions={1} | all-to-all | bytes 1048576 | tf_op jit(solution)/shard_map/all_to_all | solution.py:97
  75.6 0.2 slice_subtract_fusion.9
  75.8 0.1 reduce_window.18
  76.0 0.2 fusion.34
  76.2 0.1 broadcast_in_dim.76
  76.2 23.1 %all_to_all.11 = f32[16,4,1,512]{3,2,1,0:T(1,128)S(1)} all-to-all(f32[16,4,1,512]{3,2,1,0:T(1,128)S(1)} %broadcast_in_dim.76), channel_id=1, replica_groups=mesh['slab'=16,'swap'=64] {'slab'}, dimensions={0} | all-to-all | bytes 262144 | tf_op jit(solution)/shard_map/all_to_all | solution.py:38
  99.5 0.6 pad_maximum_fusion.6
  (19 shorter events, 0.5 us)
Async XLA Ops:
  0.6 18.7 %copy-start.1 = (f32[2,4,128,256]{3,2,1,0:T(8,128)S(1)}, f32[2,4,128,256]{3,2,1,0:T(8,128)}, u32[]{:S(2)}) copy-start(f32[2,4,128,256]{3,2,1,0:T(8,128)} %param.4) | copy-start | bytes 3145732
  0.6 18.6 %collective-permute-start = (f32[2,4,128,256]{3,2,1,0:T(8,128)}, f32[2,4,128,256]{3,2,1,0:T(8,128)S(1)}, u32[]{:S(2)}, u32[]{:S(2)}) collective-permute-start(f32[2,4,128,256]{3,2,1,0:T(8,128)} %param.4), channel_id=1, source_target_pairs={{0,1},{1,2},{2,3},{3,4},{4,5},{5,6},{6,7},{7,8},{8,9},{9,10},{10,1... | collective-permute-start | bytes 3145736 | tf_op jit(solution)/shard_map/ppermute | solution.py:18
  2.7 18.4 %collective-permute-start.1 = (f32[2,4,128,256]{3,2,1,0:T(8,128)}, f32[2,4,128,256]{3,2,1,0:T(8,128)S(1)}, u32[]{:S(2)}, u32[]{:S(2)}) collective-permute-start(f32[2,4,128,256]{3,2,1,0:T(8,128)} %param.4), channel_id=1, source_target_pairs={{1,0},{2,1},{3,2},{4,3},{5,4},{6,5},{7,6},{8,7},{9,8},{10,9},{11,1... | collective-permute-start | bytes 3145736 | tf_op jit(solution)/shard_map/ppermute | solution.py:19
  26.0 1.2 %copy-start = (f32[2,6,128,256]{3,2,1,0:T(8,128)}, f32[2,6,128,256]{3,2,1,0:T(8,128)S(1)}, u32[]{:S(2)}) copy-start(f32[2,6,128,256]{3,2,1,0:T(8,128)S(1)} %fusion.20) | copy-start | bytes 4718596
  27.4 1.2 %slice-start = ((f32[2,6,128,256]{3,2,1,0:T(8,128)}), f32[2,4,128,256]{3,2,1,0:T(8,128)S(1)}, s32[]{:S(2)}) async-start(f32[2,6,128,256]{3,2,1,0:T(8,128)} %copy-done), calls=%async_computation.2 | async-start | bytes 2097152 | tf_op jit(solution)/shard_map/slice | solution.py:57
  27.4 1.3 %copy-start.2 = (s32[4,128,256]{2,1,0:T(8,128)S(1)}, s32[4,128,256]{2,1,0:T(8,128)}, u32[]{:S(2)}) copy-start(s32[4,128,256]{2,1,0:T(8,128)} %param.5) | copy-start | bytes 1572868
where the time goes:
time: 102 us; the launch traced here: 100 us
  blocking collectives  60.8 us (60%)
  other arithmetic  15.1 us (15%)
  waiting for transfers between devices  9.54 us (9%)
  starting transfers between devices  7.8 us (8%)
  local copies, waits for them, and re-layouts  5.89 us (6%)
    all_to_all x1, blocking collectives, per_device(): lax.all_to_all(holding, 'swap', split_axis=1, concat_axis=1, tiled=True)  37.7 us
    all_to_all x1, blocking collectives, sent_to_all(): lax.all_to_all(jnp.broadcast_to(array[None], (devices, *array.shape)), ax...  23.1 us
    ppermute x1, waiting for transfers between devices, padded(): lax.ppermute(last, axis, up)  7.85 us
    div x1, other arithmetic, render_local(): optical = DEPTH_SCALE * extinction * density / total_cells  6.71 us
    ppermute x1, starting transfers between devices, padded(): lax.ppermute(leading, axis, [(b, a) for a, b in up])  5.75 us
    sub x4, other arithmetic, hydro_step(): 0.5 * (fluxes[:, :-1] + fluxes[:, 1:])  2.5 us
    ppermute x1, starting transfers between devices, padded(): lax.ppermute(last, axis, up)  2.05 us
  transfers between devices with their start and end apart: 2, of which 2 were waited for; matrix products, arithmetic and copies ran while one was open for 3% of the time, Pallas kernels for 0%

commit v1 on v0

v1 whole, which is shorter than its diff:
```python
import functools

import jax
import jax.numpy as jnp
from jax import lax
from jax.experimental import pallas as pl
from jax.experimental.pallas import tpu as pltpu
from jax.sharding import PartitionSpec as P

MESH = pl.DeviceIdType.MESH
COURANT = 0.4
DEPTH_SCALE = 2.5
STEPS = 4
LANES = 128
XS = 4
AHEAD = 8
LAG_Y = 8
LAG_X = 1


def sweep_step(rho, mom, last):
    count = len(rho)
    vel = [m / r for m, r in zip(mom, rho)]
    speed = [jnp.abs(v) for v in vel]
    flux = [m * v + r for m, v, r in zip(mom, vel, rho)]
    face_rho, face_mom = [], []
    for i in range(count - 1):
        a = jnp.maximum(speed[i], speed[i + 1]) + 1.0
        face_rho.append((mom[i] + mom[i + 1]) - a * (rho[i + 1] - rho[i]))
        if not last:
            face_mom.append((flux[i] + flux[i + 1]) - a * (mom[i + 1] - mom[i]))
    half = 0.5 * COURANT
    new_rho = [rho[i] - half * (face_rho[i] - face_rho[i - 1]) for i in range(1, count - 1)]
    new_mom = None
    if not last:
        new_mom = [mom[i] - half * (face_mom[i] - face_mom[i - 1]) for i in range(1, count - 1)]
    return new_rho, new_mom


def choose(bits, values):
    level = list(values)
    for bit in bits:
        level = [jnp.where(bit, level[2 * i + 1], level[2 * i]) for i in range(len(level) // 2)]
    return level[0]


def through_everywhere(tile, sub):
    axis = tile.ndim - 2
    only = jnp.where(sub >= 6, tile, 0.0)
    only = only + pltpu.roll(only, 4, axis)
    return only + pltpu.roll(only, 2, axis)


def over(tiles, sub):
    through = [through_everywhere(t, sub) for t in tiles]
    total = tiles[0]
    before = through[0]
    for tile, t in zip(tiles[1:], through[1:]):
        total = total + before * tile
        before = before * t
    return jnp.where(sub < 6, total, before)


def kernel(
    sizes, fluid, material, tcol, text, dens_out, image,
    own, low, high, mat, dens, part, crecv, ysrc, ybuf, xsrc, xbuf, zsrc, zbuf,
    own_sem, mat_sem, low_recv, high_recv, next_send, prev_send,
    core_send, core_recv, y_send, y_recv, x_send, x_recv, z_send, z_recv, dens_sem,
):
    zs, xs, ys = sizes
    halves = 2
    chunks = halves * xs
    layers = fluid.shape[1]
    rows = 4 * ys
    slab = lax.axis_index("slab")
    swap = lax.axis_index("swap")
    members = 2 * xs * ys
    x = swap // (2 * ys)
    y = (swap // 2) % ys
    k = swap % 2

    def member(xx, yy, kk):
        return (xx * ys + yy) * 2 + kk

    place = slab * members + swap
    after = (place + 1) % (zs * members)
    ahead = (place + zs * members - 1) % (zs * members)
    next_id = (after // members, after % members)
    prev_id = (ahead // members, ahead % members)
    partner = (slab, member(x, y, 1 - k))

    def window(ref, c):
        r = pl.multiple_of((c % xs) * rows, rows)
        col = pl.multiple_of((c // xs) * LANES, LANES)
        where = (pl.ds(r, rows), pl.ds(col, LANES))
        lead = (slice(None),) * (len(ref.shape) - 2)
        return ref.at[lead + where]

    def own_copy(c):
        return pltpu.make_async_copy(window(fluid, c), window(own, c), own_sem.at[c])

    def mat_copy(c):
        return pltpu.make_async_copy(window(material, c), window(mat, c), mat_sem.at[c])

    def dens_copy(c):
        return pltpu.make_async_copy(window(dens, c), window(dens_out, c), dens_sem.at[c])

    def remote(src, dst, send, recv, where):
        return pltpu.make_async_remote_copy(
            src_ref=src, dst_ref=dst, send_sem=send, recv_sem=recv, device_id=where, device_id_type=MESH
        )

    def to_next(c):
        return remote(window(own, c), window(low, c), next_send.at[c], low_recv.at[c], next_id)

    def to_prev(c):
        return remote(window(own, c), window(high, c), prev_send.at[c], high_recv.at[c], prev_id)

    def to_core(c):
        return remote(part.at[c, 1 - k], crecv.at[c], core_send.at[c], core_recv.at[c], partner)

    def looped(lo, hi):
        def wrap(body):
            lax.fori_loop(lo, hi, lambda i, _: (body(i), 0)[1], 0)
        return wrap

    @looped(0, chunks)
    def _(c):
        own_copy(c).start()

    @looped(0, chunks)
    def _(c):
        mat_copy(c).start()

    barrier = pltpu.get_barrier_semaphore()

    def greet(where):
        pl.semaphore_signal(barrier, inc=1, device_id=where, device_id_type=MESH)

    greet(next_id)
    greet(prev_id)
    for j in range(1, ys):
        greet((slab, member(x, (y + j) % ys, k)))
    for j in range(1, xs):
        greet((slab, member((x + j) % xs, y, k)))
    for j in range(1, zs):
        greet(((slab + j) % zs, swap))
    pl.semaphore_wait(barrier, 2 + (ys - 1) + (xs - 1) + (zs - 1))

    def send_halo(c):
        own_copy(c).wait()
        to_next(c).start()
        to_prev(c).start()

    looped(0, min(AHEAD, chunks))(send_halo)

    sub = lax.broadcasted_iota(jnp.int32, (8, LANES), 0)
    sub3 = lax.broadcasted_iota(jnp.int32, (ys, 8, LANES), 1)
    ext = [text[n] * (DEPTH_SCALE / (layers * zs * members)) for n in range(8)]
    colour = [[tcol[ch, n] for n in range(8)] for ch in range(3)]

    def compute(c):
        r0 = (c % xs) * rows
        col = pl.multiple_of((c // xs) * LANES, LANES)

        @looped(0, ys // 2)
        def _(yh):
            at = (pl.ds(pl.multiple_of(r0 + yh * 8, 8), 8), pl.ds(col, LANES))
            rho = [r[(0, i) + at] for r in (low, own, high) for i in range(layers)]
            mom = [r[(1, i) + at] for r in (low, own, high) for i in range(layers)]
            for step in range(STEPS):
                rho, mom = sweep_step(rho, mom, step == STEPS - 1)
            before = None
            total = [None] * 3
            for i in range(layers):
                dens[(i,) + at] = rho[i]
                m = mat[(i,) + at]
                bits = [(m & b) != 0 for b in (1, 2, 4)]
                through = jnp.exp(-(choose(bits, ext) * rho[i]))
                weight = 1.0 - through
                if before is not None:
                    weight = before * weight
                before = through if before is None else before * through
                for ch in range(3):
                    term = weight * choose(bits, colour[ch])
                    total[ch] = term if total[ch] is None else total[ch] + term
            a = total + [before]
            top = sub < 4
            b = [None] * 4
            for p in range(2):
                b[p] = jnp.where(top, a[p], pltpu.roll(a[p + 2], 4, 0))
                b[p + 2] = jnp.where(top, pltpu.roll(a[p], 4, 0), a[p + 2])
            even = (sub & 2) == 0
            for q in range(2):
                first, second = b[2 * q], b[2 * q + 1]
                part[c, 0, yh * 2 + q] = jnp.where(even, first, pltpu.roll(second, 2, 0))
                part[c, 1, yh * 2 + q] = jnp.where(even, pltpu.roll(first, 6, 0), second)

    def y_copy(c, j):
        other = (y + j) % ys
        return remote(ysrc.at[c, other], ybuf.at[c, y], y_send.at[c], y_recv.at[c], (slab, member(x, other, k)))

    def x_copy(c):
        return remote(xsrc.at[c], xbuf.at[c // xs, x], x_send.at[c], x_recv.at[c // xs], (slab, member(c % xs, y, k)))

    def z_copy(h, j):
        other = (slab + j) % zs
        return remote(zsrc.at[h], zbuf.at[h, slab], z_send.at[h], z_recv.at[h], (other, swap))

    def arrived(ref, sem):
        pltpu.make_async_copy(ref, ref, sem).wait()

    def first_stage(c):
        low_wait = pltpu.make_async_copy(window(low, c), window(low, c), low_recv.at[c])
        low_wait.wait()
        high_wait = pltpu.make_async_copy(window(high, c), window(high, c), high_recv.at[c])
        high_wait.wait()
        mat_copy(c).wait()
        compute(c)
        to_core(c).start()
        dens_copy(c).start()

    def core_stage(c):
        to_core(c).wait_recv()
        mine, theirs = part[c, k], crecv[c]
        is_first = k == 0
        front = jnp.where(is_first, mine, theirs)
        back = jnp.where(is_first, theirs, mine)
        both = over([front, back], sub3)
        ysrc[c] = both
        ybuf[c, y] = ysrc[c, y]
        for j in range(1, ys):
            y_copy(c, j).start()

    def y_stage(c):
        arrived(ybuf.at[c, pl.ds(0, ys - 1)], y_recv.at[c])
        done = over([ybuf[c, i] for i in range(ys)], sub)

        @pl.when(x == c % xs)
        def _():
            xbuf[c // xs, x] = done

        @pl.when(x != c % xs)
        def _():
            xsrc[c] = done
            x_copy(c).start()

    def x_stage(h):
        arrived(xbuf.at[h, pl.ds(0, xs - 1)], x_recv.at[h])
        done = over([xbuf[h, i] for i in range(xs)], sub)
        zsrc[h] = done
        zbuf[h, slab] = done
        for j in range(1, zs):
            z_copy(h, j).start()

    def z_stage(h):
        arrived(zbuf.at[h, pl.ds(0, zs - 1)], z_recv.at[h])
        done = over([zbuf[h, i] for i in range(zs)], sub)
        image[h] = jnp.where(sub < 6, done, 1.0 - done)

    @looped(0, chunks + 1 + LAG_Y + LAG_X)
    def _(t):
        @pl.when(t < chunks)
        def _():
            first_stage(t)

        if AHEAD < chunks:
            @pl.when(t + AHEAD < chunks)
            def _():
                send_halo(t + AHEAD)

        @pl.when((t >= 1) & (t < chunks + 1))
        def _():
            core_stage(t - 1)

        ty = t - 1 - LAG_Y

        @pl.when((ty >= 0) & (ty < chunks))
        def _():
            y_stage(ty)

        tx = ty - LAG_X

        @pl.when((tx >= 0) & (tx < chunks) & (x == tx % xs))
        def _():
            x_stage(tx // xs)

    for h in range(halves):
        z_stage(h)

    @looped(0, chunks)
    def _(c):
        to_next(c).wait_send()
        to_prev(c).wait_send()
        to_core(c).wait_send()
        arrived(ybuf.at[c, pl.ds(0, ys - 1)], y_send.at[c])

        @pl.when(x != c % xs)
        def _():
            x_copy(c).wait_send()

        dens_copy(c).wait()

    for h in range(halves):
        arrived(zbuf.at[h, pl.ds(0, zs - 1)], z_send.at[h])


def per_device(sizes, fluid_state, material, table_colour, table_extinction):
    zs, xs, ys = sizes
    _, layers, height, width = fluid_state.shape
    chunks = 2 * xs
    f32 = jnp.float32
    dma = pltpu.SemaphoreType.DMA
    hbm = pl.BlockSpec(memory_space=pltpu.HBM)
    vmem = pl.BlockSpec(memory_space=pltpu.VMEM)
    density, image = pl.pallas_call(
        functools.partial(kernel, sizes),
        out_shape=(
            jax.ShapeDtypeStruct((layers, height, width), f32),
            jax.ShapeDtypeStruct((2, 8, LANES), f32),
        ),
        in_specs=[hbm, hbm, pl.BlockSpec(memory_space=pltpu.SMEM), pl.BlockSpec(memory_space=pltpu.SMEM)],
        out_specs=(hbm, vmem),
        scratch_shapes=[
            pltpu.VMEM(fluid_state.shape, f32),
            pltpu.VMEM(fluid_state.shape, f32),
            pltpu.VMEM(fluid_state.shape, f32),
            pltpu.VMEM(material.shape, jnp.int32),
            pltpu.VMEM(material.shape, f32),
            pltpu.VMEM((chunks, 2, ys, 8, LANES), f32),
            pltpu.VMEM((chunks, ys, 8, LANES), f32),
            pltpu.VMEM((chunks, ys, 8, LANES), f32),
            pltpu.VMEM((chunks, ys, 8, LANES), f32),
            pltpu.VMEM((chunks, 8, LANES), f32),
            pltpu.VMEM((2, xs, 8, LANES), f32),
            pltpu.VMEM((2, 8, LANES), f32),
            pltpu.VMEM((2, zs, 8, LANES), f32),
        ]
        + [dma((chunks,))] * 11
        + [dma((2,)), dma((2,)), dma((2,)), dma((chunks,))],
        compiler_params=pltpu.CompilerParams(
            collective_id=0, has_side_effects=True, vmem_limit_bytes=65400000
        ),
        name="sweep_render",
    )(fluid_state, material, table_colour, table_extinction)
    rendered = image.reshape(2, 4, 2, LANES).transpose(1, 2, 0, 3).reshape(4, 4 * LANES)
    return density, rendered


def solution(mesh):
    slabs, members = mesh.shape["slab"], mesh.shape["swap"]
    sizes = (slabs, XS, members // (2 * XS))
    return jax.shard_map(
        functools.partial(per_device, sizes),
        mesh=mesh,
        in_specs=(P(None, ("slab", "swap"), None, None), P(("slab", "swap"), None, None), P(), P()),
        out_specs=(P(("slab", "swap"), None, None), P(None, "swap")),
        check_vma=False,
    )
```

time: 102 us -> 68.7 us (0.67); the launches traced: 100 us -> 68.4 us
  Pallas kernels: 0 us -> 64.6 us
  blocking collectives: 60.8 us -> 0 us
  other arithmetic: 15.1 us -> 0 us
  waiting for transfers between devices: 9.54 us -> 0 us
  starting transfers between devices: 7.8 us -> 0 us
  local copies, waits for them, and re-layouts: 5.89 us -> 3.19 us
    pallas_call x0 -> x1, Pallas kernels: none -> 64.6 us  [per_device(): pl.pallas_call(functools.partial(kernel, sizes), out_shape=(jax.ShapeDtyp...]
    all_to_all x2 -> x0, blocking collectives: 60.8 us -> none  [the longest x1 37.7 us: per_device(): lax.all_to_all(holding, 'swap', split_axis=1, concat_axis=1, tiled=True)]
    ppermute x2 -> x0, waiting for transfers between devices: 9.54 us -> none  [the longest x1 7.85 us: padded(): lax.ppermute(last, axis, up)]
    ppermute x2 -> x0, starting transfers between devices: 7.8 us -> none  [the longest x1 5.75 us: padded(): lax.ppermute(leading, axis, [(b, a) for a, b in up])]
    div x1 -> x0, other arithmetic: 6.71 us -> none  [render_local(): optical = DEPTH_SCALE * extinction * density / total_cells]
    slice x5 -> x0, local copies, waits for them, and re-layouts: 4.1 us -> none  [the longest x1 1.64 us: render_local(): table_extinction[number]]
    sub x12 -> x0, other arithmetic: 3.78 us -> none  [the longest x4 2.5 us: hydro_step(): 0.5 * (fluxes[:, :-1] + fluxes[:, 1:])]
    add x5 -> x0, other arithmetic: 1.99 us -> none  [the longest x4 1.41 us: hydro_step(): speeds = jnp.abs(velocity) + 1.0]
  transfers between devices with their start and end apart: 2 -> 0, of which waited for: 2 -> 0; matrix products, arithmetic and copies ran while one was open for 3% -> 0% of each run, Pallas kernels for 0% -> 0%
where the time goes in v1:
time: 68.7 us; the launch traced here: 68.4 us
  Pallas kernels  64.6 us (94%)
  local copies, waits for them, and re-layouts  3.19 us (5%)
    pallas_call x1, Pallas kernels, per_device(): pl.pallas_call(functools.partial(kernel, sizes), out_shape=(jax.ShapeDtyp...  64.6 us
    unnamed x1, local copies, waits for them, and re-layouts  1.87 us

profile of v1, /device:TPU:6, one launch (start us, length us, event | category | flops | bytes accessed | tf_op | source)
XLA Modules:
  0.0 68.4 jit_solution(1295356632328948741)
XLA Ops:
  0.6 64.6 %sweep_render.1 = (f32[4,128,256]{2,1,0:T(8,128)}, f32[2,8,128]{2,1,0:T(8,128)}) custom-call(f32[2,4,128,256]{3,2,1,0:T(8,128)} %fluid.1, s32[4,128,256]{2,1,0:T(8,128)} %material.1, f32[3,8]{1,0:T(4,128)} %tcol.1, f32[8]{0:T(128)} %text.1), custom_call_target="tpu_custom_call" | custom-call | tf_op jit(solution)/shard_map/sweep_render/pallas_call | solution.py:316
  65.2 0.7 %copy.6 = f32[4,2,2,128]{3,2,1,0:T(2,128)S(1)} copy(f32[4,2,2,128]{3,1,0,2:T(2,128)} %bitcast.3) | data formatting | bytes 16384 | tf_op jit(solution)/shard_map/transpose | solution.py:346
  65.9 0.6 reshape.11
  66.6 1.9 %copy.8 = f32[4,128,256]{2,1,0:T(8,128)} copy(f32[4,128,256]{2,1,0:T(8,128)} %get-tuple-element.8) | data formatting | bytes 1048576

commit v2 on v1

--- a/solution.py
+++ b/solution.py
@@ -15,7 +15,8 @@
 XS = 4
 AHEAD = 8
 LAG_Y = 8
-LAG_X = 1
+LAG_X = 4
+LAG_C = 1
 
 
 def sweep_step(rho, mom, last):
@@ -62,10 +63,10 @@
 
 
 def kernel(
-    sizes, fluid, material, tcol, text, dens_out, image,
-    own, low, high, mat, dens, part, crecv, ysrc, ybuf, xsrc, xbuf, zsrc, zbuf,
+    sizes, fluid, material, tcol_hbm, text_hbm, dens, image,
+    own, low, high, mat, tcol, text, part, crecv, ysrc, ybuf, xsrc, xbuf, zsrc, zbuf,
     own_sem, mat_sem, low_recv, high_recv, next_send, prev_send,
-    core_send, core_recv, y_send, y_recv, x_send, x_recv, z_send, z_recv, dens_sem,
+    core_send, core_recv, y_send, y_recv, x_send, x_recv, z_send, z_recv, table_sem, known,
 ):
     zs, xs, ys = sizes
     halves = 2
@@ -102,9 +103,6 @@
     def mat_copy(c):
         return pltpu.make_async_copy(window(material, c), window(mat, c), mat_sem.at[c])
 
-    def dens_copy(c):
-        return pltpu.make_async_copy(window(dens, c), window(dens_out, c), dens_sem.at[c])
-
     def remote(src, dst, send, recv, where):
         return pltpu.make_async_remote_copy(
             src_ref=src, dst_ref=dst, send_sem=send, recv_sem=recv, device_id=where, device_id_type=MESH
@@ -132,20 +130,47 @@
     def _(c):
         mat_copy(c).start()
 
+    tables = [
+        pltpu.make_async_copy(tcol_hbm, tcol, table_sem.at[0]),
+        pltpu.make_async_copy(text_hbm, text, table_sem.at[1]),
+    ]
+    for table in tables:
+        table.start()
+
     barrier = pltpu.get_barrier_semaphore()
 
-    def greet(where):
-        pl.semaphore_signal(barrier, inc=1, device_id=where, device_id_type=MESH)
-
-    greet(next_id)
-    greet(prev_id)
-    for j in range(1, ys):
-        greet((slab, member(x, (y + j) % ys, k)))
-    for j in range(1, xs):
-        greet((slab, member((x + j) % xs, y, k)))
-    for j in range(1, zs):
-        greet(((slab + j) % zs, swap))
-    pl.semaphore_wait(barrier, 2 + (ys - 1) + (xs - 1) + (zs - 1))
+    def around(distance, size):
+        return sorted({distance % size, -distance % size} - {0})
+
+    def along_y(distance):
+        return [(slab, member(x, (y + j) % ys, k)) for j in around(distance, ys)]
+
+    def along_x(distance):
+        return [(slab, member((x + j) % xs, y, k)) for j in around(distance, xs)]
+
+    def along_z(distance):
+        return [((slab + j) % zs, swap) for j in around(distance, zs)]
+
+    rounds = [
+        along_x(1) + along_y(1) + along_z(1),
+        along_y(2) + along_z(2),
+        along_z(4),
+    ]
+
+    def tell(sem, peers):
+        for where in peers:
+            pl.semaphore_signal(sem, inc=1, device_id=where, device_id_type=MESH)
+
+    def tell_round(n):
+        tell(known.at[n], rounds[n])
+
+    def await_round(n):
+        if rounds[n]:
+            pl.semaphore_wait(known.at[n], len(rounds[n]))
+
+    neighbours = [next_id, prev_id] + rounds[0]
+    tell(barrier, neighbours)
+    pl.semaphore_wait(barrier, len(neighbours))
 
     def send_halo(c):
         own_copy(c).wait()
@@ -153,9 +178,14 @@
         to_prev(c).start()
 
     looped(0, min(AHEAD, chunks))(send_halo)
+    tell_round(0)
+    await_round(0)
+    tell_round(1)
 
     sub = lax.broadcasted_iota(jnp.int32, (8, LANES), 0)
     sub3 = lax.broadcasted_iota(jnp.int32, (ys, 8, LANES), 1)
+    for table in tables:
+        table.wait()
     ext = [text[n] * (DEPTH_SCALE / (layers * zs * members)) for n in range(8)]
     colour = [[tcol[ch, n] for n in range(8)] for ch in range(3)]
 
@@ -218,7 +248,6 @@
         mat_copy(c).wait()
         compute(c)
         to_core(c).start()
-        dens_copy(c).start()
 
     def core_stage(c):
         to_core(c).wait_recv()
@@ -256,9 +285,13 @@
     def z_stage(h):
         arrived(zbuf.at[h, pl.ds(0, zs - 1)], z_recv.at[h])
         done = over([zbuf[h, i] for i in range(zs)], sub)
-        image[h] = jnp.where(sub < 6, done, 1.0 - done)
-
-    @looped(0, chunks + 1 + LAG_Y + LAG_X)
+        done = jnp.where(sub < 6, done, 1.0 - done)
+        for row in range(2):
+            for ch in range(4):
+                at = row * halves * LANES + h * LANES
+                image[ch : ch + 1, at : at + LANES] = done[2 * ch + row : 2 * ch + row + 1, :]
+
+    @looped(0, chunks + LAG_C + LAG_Y + LAG_X)
     def _(t):
         @pl.when(t < chunks)
         def _():
@@ -269,11 +302,20 @@
             def _():
                 send_halo(t + AHEAD)
 
-        @pl.when((t >= 1) & (t < chunks + 1))
-        def _():
-            core_stage(t - 1)
-
-        ty = t - 1 - LAG_Y
+        @pl.when(t == 1)
+        def _():
+            await_round(1)
+            tell_round(2)
+
+        @pl.when(t == 3)
+        def _():
+            await_round(2)
+
+        @pl.when((t >= LAG_C) & (t < chunks + LAG_C))
+        def _():
+            core_stage(t - LAG_C)
+
+        ty = t - LAG_C - LAG_Y
 
         @pl.when((ty >= 0) & (ty < chunks))
         def _():
@@ -298,8 +340,6 @@
         @pl.when(x != c % xs)
         def _():
             x_copy(c).wait_send()
-
-        dens_copy(c).wait()
 
     for h in range(halves):
         arrived(zbuf.at[h, pl.ds(0, zs - 1)], z_send.at[h])
@@ -317,16 +357,17 @@
         functools.partial(kernel, sizes),
         out_shape=(
             jax.ShapeDtypeStruct((layers, height, width), f32),
-            jax.ShapeDtypeStruct((2, 8, LANES), f32),
+            jax.ShapeDtypeStruct((4, 4 * LANES), f32),
         ),
-        in_specs=[hbm, hbm, pl.BlockSpec(memory_space=pltpu.SMEM), pl.BlockSpec(memory_space=pltpu.SMEM)],
-        out_specs=(hbm, vmem),
+        in_specs=[hbm] * 4,
+        out_specs=(vmem, vmem),
         scratch_shapes=[
             pltpu.VMEM(fluid_state.shape, f32),
             pltpu.VMEM(fluid_state.shape, f32),
             pltpu.VMEM(fluid_state.shape, f32),
             pltpu.VMEM(material.shape, jnp.int32),
-            pltpu.VMEM(material.shape, f32),
+            pltpu.SMEM(table_colour.shape, f32),
+            pltpu.SMEM(table_extinction.shape, f32),
             pltpu.VMEM((chunks, 2, ys, 8, LANES), f32),
             pltpu.VMEM((chunks, ys, 8, LANES), f32),
             pltpu.VMEM((chunks, ys, 8, LANES), f32),
@@ -337,14 +378,13 @@
             pltpu.VMEM((2, zs, 8, LANES), f32),
         ]
         + [dma((chunks,))] * 11
-        + [dma((2,)), dma((2,)), dma((2,)), dma((chunks,))],
+        + [dma((2,)), dma((2,)), dma((2,)), dma((2,)), pltpu.SemaphoreType.REGULAR((3,))],
         compiler_params=pltpu.CompilerParams(
-            collective_id=0, has_side_effects=True, vmem_limit_bytes=65400000
+            collective_id=0, has_side_effects=True, vmem_limit_bytes=40000000
         ),
         name="sweep_render",
-    )(fluid_state, material, table_colour, table_extinction)
-    rendered = image.reshape(2, 4, 2, LANES).transpose(1, 2, 0, 3).reshape(4, 4 * LANES)
-    return density, rendered
+    )(*[pltpu.with_memory_space_constraint(a, pltpu.HBM) for a in (fluid_state, material, table_colour, table_extinction)])
+    return density, image
 
 
 def solution(mesh):

time: 68.7 us -> 55 us (0.80)
  Pallas kernels: 64.6 us -> 52.9 us
  local copies, waits for them, and re-layouts: 3.19 us -> 1.39 us
    pallas_call x1, Pallas kernels: 64.6 us -> 52.9 us  [per_device(): pl.pallas_call(functools.partial(kernel, sizes), out_shape=(jax.ShapeDtyp...]
    transpose x1 -> x0, local copies, waits for them, and re-layouts: 0.7 us -> none  [per_device(): image.reshape(2, 4, 2, LANES).transpose(1, 2, 0, 3).reshape(4, 4 * LANES)]
    unnamed x1 -> x2, local copies, waits for them, and re-layouts: 1.87 us -> 1.39 us
where the time goes in v2:
time: 55 us; the launch traced here: 54.9 us
  Pallas kernels  52.9 us (96%)
  local copies, waits for them, and re-layouts  1.39 us (3%)
  between operations  0.64 us (1%)
    pallas_call x1, Pallas kernels, per_device(): pl.pallas_call(functools.partial(kernel, sizes), out_shape=(jax.ShapeDtyp...  52.9 us
    unnamed x2, local copies, waits for them, and re-layouts  1.39 us

profile of v2, /device:TPU:6, one launch (start us, length us, event | category | flops | bytes accessed | tf_op | source)
XLA Modules:
  0.0 54.9 jit_solution(358906982057218518)
XLA Ops:
  0.6 52.9 %sweep_render.1 = (f32[4,128,256]{2,1,0:T(8,128)S(1)}, f32[4,512]{1,0:T(4,128)S(1)}) custom-call(f32[2,4,128,256]{3,2,1,0:T(8,128)} %fluid.1, s32[4,128,256]{2,1,0:T(8,128)} %material.1, f32[3,8]{1,0:T(4,128)} %tcol_hbm.1, f32[8]{0:T(128)} %text_hbm.1), custom_call_target="tpu_custom_call" | custom-call | tf_op jit(solution)/shard_map/sweep_render/pallas_call | solution.py:356
  53.5 0.8 %copy.8 = f32[4,128,256]{2,1,0:T(8,128)} copy(f32[4,128,256]{2,1,0:T(8,128)S(1)} %get-tuple-element.4) | data formatting | bytes 1048576
  54.3 0.6 %copy.9 = f32[4,512]{1,0:T(4,128)} copy(f32[4,512]{1,0:T(4,128)S(1)} %get-tuple-element.5) | data formatting | bytes 16384

commit v3 on v2

--- a/solution.py
+++ b/solution.py
@@ -15,8 +15,6 @@
 XS = 4
 AHEAD = 8
 LAG_Y = 8
-LAG_X = 4
-LAG_C = 1
 
 
 def sweep_step(rho, mom, last):
@@ -64,9 +62,9 @@
 
 def kernel(
     sizes, fluid, material, tcol_hbm, text_hbm, dens, image,
-    own, low, high, mat, tcol, text, part, crecv, ysrc, ybuf, xsrc, xbuf, zsrc, zbuf,
+    own, low, high, mat, tcol, text, part, crecv, psrc, pbuf, zsrc, zbuf,
     own_sem, mat_sem, low_recv, high_recv, next_send, prev_send,
-    core_send, core_recv, y_send, y_recv, x_send, x_recv, z_send, z_recv, table_sem, known,
+    core_send, core_recv, plane_send, plane_recv, z_send, z_recv, table_sem, known,
 ):
     zs, xs, ys = sizes
     halves = 2
@@ -122,9 +120,55 @@
             lax.fori_loop(lo, hi, lambda i, _: (body(i), 0)[1], 0)
         return wrap
 
+    barrier = pltpu.get_barrier_semaphore()
+
+    def around(distance, size):
+        return sorted({distance % size, -distance % size} - {0})
+
+    def along_y(distance):
+        return [(slab, member(x, (y + j) % ys, k)) for j in around(distance, ys)]
+
+    def along_x(distance):
+        return [(slab, member((x + j) % xs, y, k)) for j in around(distance, xs)]
+
+    def along_z(distance):
+        return [((slab + j) % zs, swap) for j in around(distance, zs)]
+
+    rounds = [
+        along_x(1) + along_y(1) + along_z(1),
+        along_y(2) + along_z(2),
+        along_z(4) + along_x(1) + along_x(2),
+    ]
+
+    def far_first(size):
+        return sorted(range(1, size), key=lambda j: (-min(j, size - j), j))
+
+    def tell(sem, peers):
+        for where in peers:
+            pl.semaphore_signal(sem, inc=1, device_id=where, device_id_type=MESH)
+
+    def tell_round(n):
+        tell(known.at[n], rounds[n])
+
+    def await_round(n):
+        if rounds[n]:
+            pl.semaphore_wait(known.at[n], len(rounds[n]))
+
+    neighbours = [next_id, prev_id] + rounds[0]
+    tell(barrier, neighbours)
     @looped(0, chunks)
     def _(c):
         own_copy(c).start()
+
+    pl.semaphore_wait(barrier, len(neighbours))
+
+    def send_halo(c):
+        own_copy(c).wait()
+        to_next(c).start()
+        to_prev(c).start()
+
+    looped(0, min(AHEAD, chunks))(send_halo)
+    tell_round(0)
 
     @looped(0, chunks)
     def _(c):
@@ -137,48 +181,6 @@
     for table in tables:
         table.start()
 
-    barrier = pltpu.get_barrier_semaphore()
-
-    def around(distance, size):
-        return sorted({distance % size, -distance % size} - {0})
-
-    def along_y(distance):
-        return [(slab, member(x, (y + j) % ys, k)) for j in around(distance, ys)]
-
-    def along_x(distance):
-        return [(slab, member((x + j) % xs, y, k)) for j in around(distance, xs)]
-
-    def along_z(distance):
-        return [((slab + j) % zs, swap) for j in around(distance, zs)]
-
-    rounds = [
-        along_x(1) + along_y(1) + along_z(1),
-        along_y(2) + along_z(2),
-        along_z(4),
-    ]
-
-    def tell(sem, peers):
-        for where in peers:
-            pl.semaphore_signal(sem, inc=1, device_id=where, device_id_type=MESH)
-
-    def tell_round(n):
-        tell(known.at[n], rounds[n])
-
-    def await_round(n):
-        if rounds[n]:
-            pl.semaphore_wait(known.at[n], len(rounds[n]))
-
-    neighbours = [next_id, prev_id] + rounds[0]
-    tell(barrier, neighbours)
-    pl.semaphore_wait(barrier, len(neighbours))
-
-    def send_halo(c):
-        own_copy(c).wait()
-        to_next(c).start()
-        to_prev(c).start()
-
-    looped(0, min(AHEAD, chunks))(send_halo)
-    tell_round(0)
     await_round(0)
     tell_round(1)
 
@@ -226,12 +228,12 @@
                 part[c, 0, yh * 2 + q] = jnp.where(even, first, pltpu.roll(second, 2, 0))
                 part[c, 1, yh * 2 + q] = jnp.where(even, pltpu.roll(first, 6, 0), second)
 
-    def y_copy(c, j):
+    def plane_copy(c, j):
         other = (y + j) % ys
-        return remote(ysrc.at[c, other], ybuf.at[c, y], y_send.at[c], y_recv.at[c], (slab, member(x, other, k)))
-
-    def x_copy(c):
-        return remote(xsrc.at[c], xbuf.at[c // xs, x], x_send.at[c], x_recv.at[c // xs], (slab, member(c % xs, y, k)))
+        return remote(
+            psrc.at[c, other], pbuf.at[c // xs, x * ys + y], plane_send.at[c], plane_recv.at[c // xs],
+            (slab, member(c % xs, other, k)),
+        )
 
     def z_copy(h, j):
         other = (slab + j) % zs
@@ -256,30 +258,24 @@
         front = jnp.where(is_first, mine, theirs)
         back = jnp.where(is_first, theirs, mine)
         both = over([front, back], sub3)
-        ysrc[c] = both
-        ybuf[c, y] = ysrc[c, y]
-        for j in range(1, ys):
-            y_copy(c, j).start()
-
-    def y_stage(c):
-        arrived(ybuf.at[c, pl.ds(0, ys - 1)], y_recv.at[c])
-        done = over([ybuf[c, i] for i in range(ys)], sub)
+        psrc[c] = both
+        for j in far_first(ys):
+            plane_copy(c, j).start()
 
         @pl.when(x == c % xs)
         def _():
-            xbuf[c // xs, x] = done
+            pbuf[c // xs, x * ys + y] = psrc[c, y]
 
         @pl.when(x != c % xs)
         def _():
-            xsrc[c] = done
-            x_copy(c).start()
-
-    def x_stage(h):
-        arrived(xbuf.at[h, pl.ds(0, xs - 1)], x_recv.at[h])
-        done = over([xbuf[h, i] for i in range(xs)], sub)
+            plane_copy(c, 0).start()
+
+    def plane_stage(h):
+        arrived(pbuf.at[h, pl.ds(0, xs * ys - 1)], plane_recv.at[h])
+        done = over([pbuf[h, i] for i in range(xs * ys)], sub)
         zsrc[h] = done
         zbuf[h, slab] = done
-        for j in range(1, zs):
+        for j in far_first(zs):
             z_copy(h, j).start()
 
     def z_stage(h):
@@ -291,7 +287,7 @@
                 at = row * halves * LANES + h * LANES
                 image[ch : ch + 1, at : at + LANES] = done[2 * ch + row : 2 * ch + row + 1, :]
 
-    @looped(0, chunks + LAG_C + LAG_Y + LAG_X)
+    @looped(0, chunks + 1 + LAG_Y)
     def _(t):
         @pl.when(t < chunks)
         def _():
@@ -302,30 +298,24 @@
             def _():
                 send_halo(t + AHEAD)
 
-        @pl.when(t == 1)
+        @pl.when(t == 0)
         def _():
             await_round(1)
             tell_round(2)
 
-        @pl.when(t == 3)
+        @pl.when(t == 1)
         def _():
             await_round(2)
 
-        @pl.when((t >= LAG_C) & (t < chunks + LAG_C))
-        def _():
-            core_stage(t - LAG_C)
-
-        ty = t - LAG_C - LAG_Y
-
-        @pl.when((ty >= 0) & (ty < chunks))
-        def _():
-            y_stage(ty)
-
-        tx = ty - LAG_X
-
-        @pl.when((tx >= 0) & (tx < chunks) & (x == tx % xs))
-        def _():
-            x_stage(tx // xs)
+        @pl.when((t >= 1) & (t < chunks + 1))
+        def _():
+            core_stage(t - 1)
+
+        ty = t - 1 - LAG_Y
+
+        @pl.when((ty >= 0) & (ty < chunks) & (x == ty % xs))
+        def _():
+            plane_stage(ty // xs)
 
     for h in range(halves):
         z_stage(h)
@@ -335,14 +325,28 @@
         to_next(c).wait_send()
         to_prev(c).wait_send()
         to_core(c).wait_send()
-        arrived(ybuf.at[c, pl.ds(0, ys - 1)], y_send.at[c])
+
+        @pl.when(x == c % xs)
+        def _():
+            arrived(pbuf.at[0, pl.ds(0, ys - 1)], plane_send.at[c])
 
         @pl.when(x != c % xs)
         def _():
-            x_copy(c).wait_send()
+            arrived(pbuf.at[0, pl.ds(0, ys)], plane_send.at[c])
 
     for h in range(halves):
         arrived(zbuf.at[h, pl.ds(0, zs - 1)], z_send.at[h])
+
+
+def put(dens, image, dens_out, image_out, sems):
+    copies = [
+        pltpu.make_async_copy(dens, dens_out, sems.at[0]),
+        pltpu.make_async_copy(image, image_out, sems.at[1]),
+    ]
+    for copy in copies:
+        copy.start()
+    for copy in copies:
+        copy.wait()
 
 
 def per_device(sizes, fluid_state, material, table_colour, table_extinction):
@@ -371,20 +375,26 @@
             pltpu.VMEM((chunks, 2, ys, 8, LANES), f32),
             pltpu.VMEM((chunks, ys, 8, LANES), f32),
             pltpu.VMEM((chunks, ys, 8, LANES), f32),
-            pltpu.VMEM((chunks, ys, 8, LANES), f32),
-            pltpu.VMEM((chunks, 8, LANES), f32),
-            pltpu.VMEM((2, xs, 8, LANES), f32),
+            pltpu.VMEM((2, xs * ys, 8, LANES), f32),
             pltpu.VMEM((2, 8, LANES), f32),
             pltpu.VMEM((2, zs, 8, LANES), f32),
         ]
-        + [dma((chunks,))] * 11
-        + [dma((2,)), dma((2,)), dma((2,)), dma((2,)), pltpu.SemaphoreType.REGULAR((3,))],
+        + [dma((chunks,))] * 9
+        + [dma((2,))] * 4
+        + [pltpu.SemaphoreType.REGULAR((3,))],
         compiler_params=pltpu.CompilerParams(
             collective_id=0, has_side_effects=True, vmem_limit_bytes=40000000
         ),
         name="sweep_render",
     )(*[pltpu.with_memory_space_constraint(a, pltpu.HBM) for a in (fluid_state, material, table_colour, table_extinction)])
-    return density, image
+    return pl.pallas_call(
+        put,
+        out_shape=(pltpu.HBM(density.shape, f32), pltpu.HBM(image.shape, f32)),
+        in_specs=[vmem, vmem],
+        out_specs=(hbm, hbm),
+        scratch_shapes=[dma((2,))],
+        name="put",
+    )(*[pltpu.with_memory_space_constraint(a, pltpu.VMEM) for a in (density, image)])
 
 
 def solution(mesh):

time: 55 us -> 52 us (0.945)
  Pallas kernels: 52.9 us -> 51.1 us
  local copies, waits for them, and re-layouts: 1.39 us -> 0 us
    pallas_call x1, Pallas kernels: 52.9 us -> 50.3 us  [per_device(): pl.pallas_call(functools.partial(kernel, sizes), out_shape=(jax.ShapeDtyp...]
    unnamed x2 -> x0, local copies, waits for them, and re-layouts: 1.39 us -> none
    pallas_call x0 -> x1, Pallas kernels: none -> 0.81 us  [per_device(): pl.pallas_call(put, out_shape=(pltpu.HBM(density.shape, f32), pltpu.HBM(i...]
where the time goes in v3:
time: 52 us; the launch traced here: 51.8 us
  Pallas kernels  51.1 us (98%)
  between operations  0.64 us (1%)
    pallas_call x1, Pallas kernels, per_device(): pl.pallas_call(functools.partial(kernel, sizes), out_shape=(jax.ShapeDtyp...  50.3 us

profile of v3, /device:TPU:6, one launch (start us, length us, event | category | flops | bytes accessed | tf_op | source)
XLA Modules:
  0.0 51.8 jit_solution(9081331775193912012)
XLA Ops:
  0.6 50.3 %sweep_render.1 = (f32[4,128,256]{2,1,0:T(8,128)S(1)}, f32[4,512]{1,0:T(4,128)S(1)}) custom-call(f32[2,4,128,256]{3,2,1,0:T(8,128)} %fluid.1, s32[4,128,256]{2,1,0:T(8,128)} %material.1, f32[3,8]{1,0:T(4,128)} %tcol_hbm.1, f32[8]{0:T(128)} %text_hbm.1), custom_call_target="tpu_custom_call" | custom-call | tf_op jit(solution)/shard_map/sweep_render/pallas_call | solution.py:360
  51.0 0.8 %put.1 = (f32[4,128,256]{2,1,0:T(8,128)}, f32[4,512]{1,0:T(4,128)}) custom-call(f32[4,128,256]{2,1,0:T(8,128)S(1)} %get-tuple-element.4.dens, f32[4,512]{1,0:T(4,128)S(1)} %get-tuple-element.5.image), custom_call_target="tpu_custom_call" | custom-call | tf_op jit(solution)/shard_map/put/pallas_call | solution.py:390

commit v4 on v3

--- a/solution.py
+++ b/solution.py
@@ -317,9 +317,6 @@
         def _():
             plane_stage(ty // xs)
 
-    for h in range(halves):
-        z_stage(h)
-
     @looped(0, chunks)
     def _(c):
         to_next(c).wait_send()
@@ -333,6 +330,9 @@
         @pl.when(x != c % xs)
         def _():
             arrived(pbuf.at[0, pl.ds(0, ys)], plane_send.at[c])
+
+    for h in range(halves):
+        z_stage(h)
 
     for h in range(halves):
         arrived(zbuf.at[h, pl.ds(0, zs - 1)], z_send.at[h])

time: 52 us -> 51.8 us (level)
  no operation moved by 1% of the time
where the time goes in v4:
time: 51.8 us; the launch traced here: 51.7 us
  Pallas kernels  51 us (98%)
  between operations  0.64 us (1%)
    pallas_call x1, Pallas kernels, per_device(): pl.pallas_call(functools.partial(kernel, sizes), out_shape=(jax.ShapeDtyp...  50.2 us

profile of v4, /device:TPU:6, one launch (start us, length us, event | category | flops | bytes accessed | tf_op | source)
XLA Modules:
  0.0 51.7 jit_solution(3730217571566853268)
XLA Ops:
  0.6 50.2 %sweep_render.1 = (f32[4,128,256]{2,1,0:T(8,128)S(1)}, f32[4,512]{1,0:T(4,128)S(1)}) custom-call(f32[2,4,128,256]{3,2,1,0:T(8,128)} %fluid.1, s32[4,128,256]{2,1,0:T(8,128)} %material.1, f32[3,8]{1,0:T(4,128)} %tcol_hbm.1, f32[8]{0:T(128)} %text_hbm.1), custom_call_target="tpu_custom_call" | custom-call | tf_op jit(solution)/shard_map/sweep_render/pallas_call | solution.py:360
  50.8 0.8 %put.1 = (f32[4,128,256]{2,1,0:T(8,128)}, f32[4,512]{1,0:T(4,128)}) custom-call(f32[4,128,256]{2,1,0:T(8,128)S(1)} %get-tuple-element.4.dens, f32[4,512]{1,0:T(4,128)S(1)} %get-tuple-element.5.image), custom_call_target="tpu_custom_call" | custom-call | tf_op jit(solution)/shard_map/put/pallas_call | solution.py:390
